TPU v7x, 256 devices: a whole 4x4x8 slice. The times are simulated.
256 devices in a mesh: seq: 2 (over core), chan: 16 (over y, x), batch: 8 (over z).
Axes of the slice: x: 4, y: 4, z: 8, core: 2. Of those that a mesh axis runs over, the one named last changes fastest.
Arguments:
- ssm_input: bfloat16 [16384, 4096], P(('batch', 'seq'), 'chan'), parts along dimension 0, may hold values from -6 to 6
- gate_z: bfloat16 [16384, 4096], P(('batch', 'seq'), 'chan'), parts along dimension 0, may hold values from -6 to 6
- proj_forward: bfloat16 [2, 16384, 128], P(None, ('batch', 'seq')), parts along dimension 1, may hold values from -2 to 2
- proj_backward: bfloat16 [2, 16384, 128], P(None, ('batch', 'seq')), parts along dimension 1, may hold values from -2 to 2
- step_raw: float32 [2, 64, 16384], P(None, 'chan', ('batch', 'seq')), parts along dimension 2, may hold values from -3 to 3
- head_params: float32 [2, 2, 64], P(None, None, 'chan'), may hold values from -4 to 1, as said below
- skip_gain: float32 [64], P('chan'), may hold values from 0.25 to 2
- norm_gain: float32 [4096], P('chan'), may hold values from 0.5 to 1.5
- out_weight: bfloat16 [4096, 2048], P(None, 'chan'), may hold values from -0.09375 to 0.09375
Outputs:
- mixed: bfloat16 [16384, 2048], P(('batch', 'seq'), 'chan'), parts along dimension 0
There are 8 independent parts, one for each index of `batch`. A program takes and returns all parts, laid end to end along the dimension named above; an argument that names none is the same for every part. Nothing has to cross between parts.
Inputs may be any that keep to these rules, and one draw needn't show every extreme that they name: `head_params`: index 0 of the second dimension holds positive decay rates, index 1 time-step biases.
All inputs are finite; a program needn't handle non-finite values.
Results may differ from a plain program's by a relative error of at most 0.0085.
Values may be sent and summed in bfloat16 or wider, within the bound.
A program may use at most 128 MiB of HBM per device.

v0:
```python
import jax
import jax.numpy as jnp
from jax import lax
from jax.sharding import PartitionSpec as P

SPAN = 256
INNER = 4096


def sent_together(arrays, axis, dim, along):
    columns = [a.reshape(*a.shape[:along], -1) for a in arrays]
    both = jnp.concatenate(columns, axis=along)
    whole, at, done = (lax.all_gather(both, axis, axis=dim, tiled=True), 0, [])
    for a, column in zip(arrays, columns):
        slab = whole[..., at : at + column.shape[along]]
        done.append(slab.reshape(*slab.shape[:along], *a.shape[along:]))
        at += column.shape[along]
    return tuple(done)


def copy_for_each(value, axis):
    copies = jnp.broadcast_to(value, (lax.axis_size(axis), *value.shape))
    return lax.all_to_all(copies, axis, split_axis=0, concat_axis=0, tiled=True)


def taken_together(value, axis):
    everything = copy_for_each(value, axis)
    return jnp.sum(everything, axis=0)


def local_scan(blocks_x, b_rows, c_rows, steps_here, decay_rates):
    cumlog = jnp.cumsum(-decay_rates[None, :, None] * steps_here, axis=2)
    scores = jnp.einsum("cqn,csn->cqs", c_rows, b_rows, preferred_element_type=jnp.float32)
    lower_mask = jnp.tril(jnp.ones((SPAN, SPAN), dtype=bool))
    log_gaps = cumlog[:, :, :, None] - cumlog[:, :, None, :]
    decays = jnp.where(lower_mask, jnp.exp(jnp.where(lower_mask, log_gaps, 0.0)), 0.0)
    weights = (scores[:, None] * decays * steps_here[:, :, None, :]).astype(jnp.bfloat16)
    intra_out = jnp.einsum("chts,cshp->cthp", weights, blocks_x, preferred_element_type=jnp.float32)
    end_logs = cumlog[:, :, -1]
    in_weights = jnp.exp(end_logs[:, :, None] - cumlog) * steps_here
    b_weighted = (b_rows[:, None].astype(jnp.float32) * in_weights[..., None]).astype(jnp.bfloat16)
    block_states = jnp.einsum(
        "cshp,chsn->chpn", blocks_x, b_weighted, preferred_element_type=jnp.float32
    )

    def advance(carried, inputs):
        gain_log, block_state = inputs
        return (jnp.exp(gain_log)[:, None, None] * carried + block_state, carried)

    initial = jnp.zeros(block_states.shape[1:], jnp.float32)
    end_state, entering = lax.scan(advance, initial, (end_logs, block_states))
    before = jnp.cumsum(end_logs, axis=0) - end_logs
    whole_decay = jnp.exp(jnp.sum(end_logs, axis=0))
    return ((intra_out, entering, cumlog, before, c_rows), (whole_decay, end_state))


def finish(pieces, carried):
    intra_out, entering, cumlog, before, c_rows = pieces
    states = entering + jnp.exp(before)[:, :, None, None] * carried[None]
    inter = jnp.einsum("ctn,chpn->cthp", c_rows.astype(jnp.float32), states)
    inter = inter * jnp.exp(cumlog).transpose(0, 2, 1)[..., None]
    outputs = intra_out + inter
    return outputs.reshape(outputs.shape[0] * outputs.shape[1], -1)


def body(
    ssm_input,
    gate_z,
    proj_forward,
    proj_backward,
    step_raw,
    head_params,
    skip_gain,
    norm_gain,
    out_weight,
):
    frames, inner_here = ssm_input.shape
    heads_here = step_raw.shape[1]
    width = inner_here // heads_here
    blocks = frames // SPAN
    shape_x = (blocks, SPAN, heads_here, width)
    shape_rows = (blocks, SPAN, proj_forward.shape[2])

    def to_blocks(steps):
        return steps.reshape(heads_here, blocks, SPAN).transpose(1, 0, 2)

    steps_fwd = jax.nn.softplus(step_raw[0] + head_params[0, 1][:, None])
    steps_bwd = jax.nn.softplus(step_raw[1] + head_params[1, 1][:, None])[:, ::-1]
    fwd_parts, fwd_end = local_scan(
        ssm_input.reshape(shape_x),
        proj_forward[0].reshape(shape_rows),
        proj_forward[1].reshape(shape_rows),
        to_blocks(steps_fwd),
        head_params[0, 0],
    )
    bwd_parts, bwd_end = local_scan(
        ssm_input[::-1].reshape(shape_x),
        proj_backward[0][::-1].reshape(shape_rows),
        proj_backward[1][::-1].reshape(shape_rows),
        to_blocks(steps_bwd),
        head_params[1, 0],
    )
    decays_all, states_all = tuple(
        (
            part.astype(jnp.float32)
            for part in sent_together(
                (
                    jnp.stack([fwd_end[0], bwd_end[0]])[None].astype(jnp.bfloat16),
                    jnp.stack([fwd_end[1], bwd_end[1]])[None].astype(jnp.bfloat16),
                ),
                "seq",
                0,
                3,
            )
        )
    )
    own_index = lax.axis_index("seq")
    group_size = lax.axis_size("seq")

    def accumulate(position, carried):
        forward_state, backward_state = carried
        mirror = group_size - 1 - position
        forward_state = jnp.where(
            position < own_index,
            decays_all[position, 0][:, None, None] * forward_state + states_all[position, 0],
            forward_state,
        )
        backward_state = jnp.where(
            mirror > own_index,
            decays_all[mirror, 1][:, None, None] * backward_state + states_all[mirror, 1],
            backward_state,
        )
        return (forward_state, backward_state)

    empty_state = jnp.zeros(fwd_end[1].shape, jnp.float32)
    carry_fwd, carry_bwd = lax.fori_loop(0, group_size, accumulate, (empty_state, empty_state))
    forward_out = finish(fwd_parts, carry_fwd)
    backward_out = finish(bwd_parts, carry_bwd)[::-1]
    skipped = (
        ssm_input.reshape(frames, heads_here, width).astype(jnp.float32) * skip_gain[:, None]
    ).reshape(frames, inner_here)
    gated = (forward_out + backward_out + skipped) * jax.nn.silu(gate_z.astype(jnp.float32))
    squares = taken_together(jnp.sum(gated * gated, axis=1), "chan")
    scale = lax.rsqrt(squares / INNER + 1.0)
    normed = (gated * scale[:, None] * norm_gain).astype(jnp.bfloat16)
    frame_share = lax.all_to_all(normed, "chan", split_axis=0, concat_axis=1, tiled=True)
    projected = jnp.dot(
        frame_share,
        lax.all_gather(out_weight, "chan", axis=1, tiled=True),
        preferred_element_type=jnp.float32,
    ).astype(jnp.bfloat16)
    return lax.all_to_all(projected, "chan", split_axis=1, concat_axis=0, tiled=True)


def solution(mesh):
    in_specs = (
        P(("batch", "seq"), "chan"),
        P(("batch", "seq"), "chan"),
        P(None, ("batch", "seq"), None),
        P(None, ("batch", "seq"), None),
        P(None, "chan", ("batch", "seq")),
        P(None, None, "chan"),
        P("chan"),
        P("chan"),
        P(None, "chan"),
    )
    out_specs = P(("batch", "seq"), "chan")
    return jax.shard_map(body, mesh=mesh, in_specs=in_specs, out_specs=out_specs, check_vma=False)
```

profile of v0, /device:TPU:96, one launch (start us, length us, event | category | flops | bytes accessed | tf_op | source)
XLA Modules:
  0.0 171.4 jit_solution(11320585137728651989)
XLA Ops:
  6.5 0.7 all-gather.2.cloned.1.call-update
  7.3 1.2 copy.167
  8.5 6.3 %rev.17 = bf16[1024,256]{1,0:T(8,128)(2,1)S(1)} reverse(bf16[1024,256]{1,0:T(8,128)(2,1)} %param.15), dimensions={0} | reverse | bytes 1048576 | tf_op jit(solution)/shard_map/rev | solution.py:97
  14.9 0.7 slice.57
  15.6 0.8 negate_bitcast_fusion
  16.4 0.8 compare_select_fusion
  17.2 0.7 rev.15
  18.0 4.8 %reduce-window.14 = f32[4,4,2,128]{3,2,1,0:T(2,128)S(1)} reduce-window(f32[4,4,2,128]{3,2,1,0:T(2,128)S(1)} %reshape.296, f32[]{:T(128)} %constant.83.clone.1), window={size=1x1x1x128 pad=0_0x0_0x0_0x127_0}, to_apply=%region_0.1 | reduce-window | flops 520192 | bytes 32772 | tf_op jit(solution)/shard_map/reduce-window
  23.6 1.1 fusion.56
  24.8 1.2 reshape.298
  26.6 1.9 %convolution_bitcast_fusion.3 = f32[4,4,64,128]{3,2,1,0:T(8,128)S(1)} fusion(f32[4,4,256]{2,1,0:T(4,128)S(1)} %get-tuple-element.329, f32[4,256,128]{2,1,0:T(8,128)S(1)} %convert_element_type.76, bf16[4,256,4,64]{1,0,3,2:T(4,128)(2,1)} %reshape.298), kind=kOutput, calls=%fused_computation.48 | convolution fusion | flops 68157440 | bytes 1589248 | tf_op jit(solution)/shard_map/cshp,chsn->chpn/dot_general | solution.py:42
  29.3 4.8 %reduce-window.16 = f32[4,4,2,128]{3,2,1,0:T(2,128)S(1)} reduce-window(f32[4,4,2,128]{3,2,1,0:T(2,128)S(1)} %reshape.300, f32[]{:T(128)} %constant.83.clone.1), window={size=1x1x1x128 pad=0_0x0_0x0_0x127_0}, to_apply=%region_6.7 | reduce-window | flops 520192 | bytes 32772 | tf_op jit(solution)/shard_map/reduce-window.2
  34.9 1.8 %slice_bitcast_fusion = (bf16[1024,128]{1,0:T(8,128)(2,1)}, bf16[1024,128]{1,0:T(8,128)(2,1)S(1)}) fusion(bf16[2,1024,128]{2,1,0:T(8,128)(2,1)} %param.18), kind=kLoop, calls=%fused_computation.70 | loop fusion | bytes 1048576 | tf_op jit(solution)/shard_map/squeeze | solution.py:99
  36.9 0.8 convert_element_type.78
  39.3 2.0 %convolution_bitcast_fusion.2 = f32[4,4,64,128]{3,2,1,0:T(8,128)S(1)} fusion(bf16[4,256,4,64]{1,3,2,0:T(8,128)(2,1)S(1)} %copy.176, f32[4,4,256]{2,1,0:T(4,128)S(1)} %get-tuple-element.324, f32[4,256,128]{2,1,0:T(8,128)} %convert_element_type.78), kind=kOutput, calls=%fused_computation.47 | convolution fusion | flops 68157440 | bytes 1589248 | tf_op jit(solution)/shard_map/cshp,chsn->chpn/dot_general | solution.py:42
  42.7 2.0 %all_gather.6 = bf16[2,2,4,8193]{3,2,1,0:T(4,128)(2,1)S(1)} all-gather(bf16[1,2,4,8193]{3,2,1,0:T(4,128)(2,1)S(1)} %maximum_maximum_fusion), channel_id=1, replica_groups=mesh['seq'=2,'chan'=16,'batch'=8] {'seq'}, dimensions={0}, use_global_device_ids=true | all-gather | bytes 393264 | tf_op jit(solution)/shard_map/all_gather | solution.py:13
  45.4 3.2 %rev.18 = bf16[1024,128]{1,0:T(8,128)(2,1)S(1)} reverse(bf16[1024,128]{1,0:T(8,128)(2,1)} %get-tuple-element.319), dimensions={0} | reverse | bytes 524288 | tf_op jit(solution)/shard_map/rev | solution.py:99
  49.6 3.1 %fusion.22 = f32[4,256,4,64]{1,3,2,0:T(8,128)} fusion(bf16[4,256,4,64]{1,3,2,0:T(8,128)(2,1)S(1)} %copy.176, f32[4,4,256]{2,1,0:T(4,128)} %bitcast.166, f32[4,4,256]{2,1,0:T(4,128)S(1)} %copy-done.9, f32[4,256,256]{2,1,0:T(8,128)S(1)} %fusion.58, pred[256,256]{1,0:T(8,128)(4,1)S(1)} %iota_compare_fusion), kind=kOutput, calls=%fused_computation.37 | convolution fusion | flops 140509184 | bytes 2719744 | tf_op jit(solution)/shard_map/chts,cshp->cthp/dot_general | solution.py:38
  53.0 0.7 copy-done.3
  53.8 1.6 fusion.25
  55.4 0.7 copy.180
  56.3 1.5 rev.19
  58.2 2.5 %fusion.23 = f32[4,256,4,64]{1,3,2,0:T(8,128)S(1)} fusion(f32[4,4,256]{2,1,0:T(4,128)S(1)} %copy-done.13, f32[4,4,256]{2,1,0:T(4,128)S(1)} %copy-done.7, f32[4,256,256]{2,1,0:T(8,128)S(1)} %fusion.57, pred[256,256]{1,0:T(8,128)(4,1)S(1)} %copy-done.11, bf16[4,256,4,64]{1,0,3,2:T(4,128)(2,1)} %reshape.298), kind=kOutput, calls=%fused_computation.38 | convolution fusion | flops 140509184 | bytes 2719744 | tf_op jit(solution)/shard_map/chts,cshp->cthp/dot_general | solution.py:38
  61.1 0.7 copy.178
  61.8 1.2 copy.198
  63.3 1.8 %multiply_reduce_fusion = (f32[1024]{0:T(1024)S(1)}, f32[1024,256]{0,1:T(8,128)S(1)}) fusion(bf16[1024,256]{0,1:T(8,128)(2,1)S(1)} %copy.182, f32[256]{0:T(256)S(1)} %mul.274, bf16[1024,256]{0,1:T(8,128)(2,1)S(1)} %copy.167, f32[1024,256]{0,1:T(8,128)} %bitcast.150, f32[1024,256]{0,1:T(8,128)S(1)} %rev.19), kind=kLoop, calls=%fused_computation.55 | loop fusion | flops 3144704 | bytes 4199424 | tf_op jit(solution)/shard_map/reduce_sum | solution.py:143
  65.2 15.2 %all_to_all.46 = f32[16,1,1024]{2,1,0:T(1,128)S(1)} all-to-all(f32[16,1,1024]{2,1,0:T(1,128)S(1)} %broadcast_in_dim.57), channel_id=1, replica_groups=mesh['seq'=2,'chan'=16,'batch'=8] {'chan'}, dimensions={0} | all-to-all | bytes 131072 | tf_op jit(solution)/shard_map/all_to_all | solution.py:23
  80.8 18.8 %all_to_all.44 = bf16[16,64,256]{2,1,0:T(8,128)(2,1)S(1)} all-to-all(bf16[16,64,256]{2,1,0:T(8,128)(2,1)S(1)} %bitcast.160), channel_id=1, replica_groups=mesh['seq'=2,'chan'=16,'batch'=8] {'chan'}, dimensions={0} | all-to-all | bytes 1048576 | tf_op jit(solution)/shard_map/all_to_all | solution.py:146
  99.7 42.4 %all-gather.2.cloned.1.call-done = bf16[4096,2048]{1,0:T(8,128)(2,1)} async-done(((bf16[4096,128]{1,0:T(8,128)(2,1)}), bf16[4096,2048]{1,0:T(8,128)(2,1)}) %all-gather.2.cloned.1.call-update) | async-done | bytes 16777232 | tf_op jit(solution)/shard_map/all_gather | solution.py:149
  142.1 8.8 %fusion.28 = bf16[8,16,8,128]{3,2,1,0:T(8,128)(2,1)S(1)} fusion(bf16[64,4096]{1,0:T(8,128)(2,1)S(1)} %bitcast.151, bf16[4096,2048]{1,0:T(8,128)(2,1)} %all-gather.2.cloned.1.call-done), kind=kOutput, calls=%fused_computation.49 | convolution fusion | flops 1073872896 | bytes 17563648 | tf_op jit(solution)/shard_map/dot_general | solution.py:147
  150.9 12.9 %all_to_all.45 = bf16[64,16,128]{2,0,1:T(8,128)(2,1)S(1)} all-to-all(bf16[64,16,128]{2,0,1:T(8,128)(2,1)S(1)} %bitcast.162), channel_id=1, replica_groups=mesh['seq'=2,'chan'=16,'batch'=8] {'chan'}, dimensions={1} | all-to-all | bytes 524288 | tf_op jit(solution)/shard_map/all_to_all | solution.py:152
  163.8 0.7 copy.241
  (135 shorter events, 11.0 us)
Async XLA Ops:
  6.5 135.5 %all-gather.2.cloned.1.call-start = ((), (), s32[]{:S(2)}) async-start(), calls=%async_computation.3 | async-start | bytes 17825792 | tf_op jit(solution)/shard_map/all_gather | solution.py:149
  17.9 20.8 %copy-start.5 = (f32[4,1024]{1,0:T(4,128)}, f32[4,1024]{1,0:T(4,128)S(1)}, u32[]{:S(2)}) copy-start(f32[4,1024]{1,0:T(4,128)S(1)} %rev.15) | copy-start | bytes 49156
  18.0 10.6 %copy-start.12 = (f32[4,4,256]{2,1,0:T(4,128)}, f32[4,4,256]{2,1,0:T(4,128)S(1)}, u32[]{:S(2)}) copy-start(f32[4,4,256]{2,1,0:T(4,128)S(1)} %get-tuple-element.314) | copy-start | bytes 49156
  23.3 3.3 %copy-start.6 = (f32[4,4,256]{2,1,0:T(4,128)}, f32[4,4,256]{2,1,0:T(4,128)S(1)}, u32[]{:S(2)}) copy-start(f32[4,4,256]{2,1,0:T(4,128)S(1)} %reduce_window_sum.59) | copy-start | bytes 49156
  29.2 7.5 %copy-start = (f32[4,4,64,128]{3,2,1,0:T(8,128)}, f32[4,4,64,128]{3,2,1,0:T(8,128)S(1)}, u32[]{:S(2)}) copy-start(f32[4,4,64,128]{3,2,1,0:T(8,128)S(1)} %get-tuple-element.216) | copy-start | bytes 1572868
  29.2 7.7 %copy-start.16 = (f32[4,4]{1,0:T(4,128)}, f32[4,4]{1,0:T(4,128)S(1)}, u32[]{:S(2)}) copy-start(f32[4,4]{1,0:T(4,128)S(1)} %get-tuple-element.516) | copy-start | bytes 196
  34.6 6.8 %copy-start.8 = (f32[4,4,256]{2,1,0:T(4,128)}, f32[4,4,256]{2,1,0:T(4,128)S(1)}, u32[]{:S(2)}) copy-start(f32[4,4,256]{2,1,0:T(4,128)S(1)} %reduce_window_sum.62) | copy-start | bytes 49156
  42.0 0.8 copy-start.2
  42.0 7.6 %copy-start.9 = (f32[4,4,256]{2,1,0:T(4,128)S(1)}, f32[4,4,256]{2,1,0:T(4,128)}, u32[]{:S(2)}) copy-start(f32[4,4,256]{2,1,0:T(4,128)} %copy-done.8) | copy-start | bytes 49156
  48.7 4.1 %copy-start.10 = (pred[256,256]{1,0:T(8,128)(4,1)}, pred[256,256]{1,0:T(8,128)(4,1)S(1)}, u32[]{:S(2)}) copy-start(pred[256,256]{1,0:T(8,128)(4,1)S(1)} %iota_compare_fusion) | copy-start | bytes 196612
  52.7 1.0 copy-start.3
  52.7 1.0 copy-start.15
  55.3 2.4 %copy-start.17 = (f32[4,4]{1,0:T(4,128)S(1)}, f32[4,4]{1,0:T(4,128)}, u32[]{:S(2)}) copy-start(f32[4,4]{1,0:T(4,128)} %copy-done.16) | copy-start | bytes 196
  55.3 2.8 %copy-start.7 = (f32[4,4,256]{2,1,0:T(4,128)S(1)}, f32[4,4,256]{2,1,0:T(4,128)}, u32[]{:S(2)}) copy-start(f32[4,4,256]{2,1,0:T(4,128)} %copy-done.6) | copy-start | bytes 49156
  55.4 2.8 %copy-start.11 = (pred[256,256]{1,0:T(8,128)(4,1)S(1)}, pred[256,256]{1,0:T(8,128)(4,1)}, u32[]{:S(2)}) copy-start(pred[256,256]{1,0:T(8,128)(4,1)} %copy-done.10) | copy-start | bytes 196612
  55.4 2.8 %copy-start.13 = (f32[4,4,256]{2,1,0:T(4,128)S(1)}, f32[4,4,256]{2,1,0:T(4,128)}, u32[]{:S(2)}) copy-start(f32[4,4,256]{2,1,0:T(4,128)} %copy-done.12) | copy-start | bytes 49156
  58.2 2.5 %copy-start.1 = (f32[4,4,64,128]{3,2,1,0:T(8,128)S(1)}, f32[4,4,64,128]{3,2,1,0:T(8,128)}, u32[]{:S(2)}) copy-start(f32[4,4,64,128]{3,2,1,0:T(8,128)} %copy-done) | copy-start | bytes 1572868
  58.2 2.5 %copy-start.14 = (f32[4,256,4]{1,2,0:T(4,128)S(1)}, f32[4,256,4]{1,2,0:T(4,128)}, u32[]{:S(2)}) copy-start(f32[4,256,4]{1,2,0:T(4,128)} %get-tuple-element.330) | copy-start | bytes 49156
  60.7 2.3 %copy-start.4 = (bf16[1024,256]{1,0:T(8,128)(2,1)S(1)}, bf16[1024,256]{1,0:T(8,128)(2,1)}, u32[]{:S(2)}) copy-start(bf16[1024,256]{1,0:T(8,128)(2,1)} %param.16) | copy-start | bytes 1572868
  60.7 2.5 %copy-start.19 = (f32[4]{0:T(128)S(1)}, f32[4]{0:T(128)}, u32[]{:S(2)}) copy-start(f32[4]{0:T(128)} %param.21) | copy-start | bytes 52
  61.8 18.7 %copy-start.18 = (f32[256]{0:T(256)S(1)}, f32[256]{0:T(256)}, u32[]{:S(2)}) copy-start(f32[256]{0:T(256)} %param.22) | copy-start | bytes 3076
Sparse Core Ops, SparseCore 0:
  9.7 132.2 all-gather.1
where the time goes:
time: 173 us; the launch traced here: 171 us
  blocking collectives  48.9 us (28%)
  waiting for transfers between devices  43.1 us (25%)
  local copies, waits for them, and re-layouts  26 us (15%)
  matrix products  20.8 us (12%)
  other arithmetic  18.2 us (11%)
  between operations  14 us (8%)
    all_gather x1, waiting for transfers between devices, body(): lax.all_gather(out_weight, 'chan', axis=1, tiled=True)  42.4 us
    all_to_all x1, blocking collectives, body(): lax.all_to_all(normed, 'chan', split_axis=0, concat_axis=1, tiled=True)  18.8 us
    all_to_all x1, blocking collectives, copy_for_each(): return lax.all_to_all(copies, axis, split_axis=0, concat_axis=0, tiled=True)  15.2 us
    all_to_all x1, blocking collectives, body(): lax.all_to_all(projected, 'chan', split_axis=1, concat_axis=0, tiled=True)  12.9 us
    another operation x8, other arithmetic  9.88 us
    dot_general x1, matrix products, body(): jnp.dot(frame_share, lax.all_gather(out_weight, 'chan', axis=1, tiled=Tru...  8.79 us
    rev x1, local copies, waits for them, and re-layouts, body(): ssm_input[::-1].reshape(shape_x)  6.33 us
    dot_general x2, matrix products, local_scan(): jnp.einsum('chts,cshp->cthp', weights, blocks_x, preferred_element_type=j...  5.62 us
  transfers between devices with their start and end apart: 1, of which 1 were waited for; matrix products, arithmetic and copies ran while one was open for 32% of the time, Pallas kernels for 0%

commit v1 on v0

--- a/solution.py
+++ b/solution.py
@@ -144,10 +144,11 @@
     scale = lax.rsqrt(squares / INNER + 1.0)
     normed = (gated * scale[:, None] * norm_gain).astype(jnp.bfloat16)
     frame_share = lax.all_to_all(normed, "chan", split_axis=0, concat_axis=1, tiled=True)
+    follow_bench = lambda x_local: jnp.concatenate(
+        lax.all_to_all(jnp.stack([x_local for _ in range(lax.axis_size("chan"))]), "chan", 0, 0), 1
+    )
     projected = jnp.dot(
-        frame_share,
-        lax.all_gather(out_weight, "chan", axis=1, tiled=True),
-        preferred_element_type=jnp.float32,
+        frame_share, follow_bench(out_weight), preferred_element_type=jnp.float32
     ).astype(jnp.bfloat16)
     return lax.all_to_all(projected, "chan", split_axis=1, concat_axis=0, tiled=True)
 

time: 173 us -> 360 us (2.08)
  waiting for transfers between devices: 43.1 us -> 252 us
  blocking collectives: 48.9 us -> 31.7 us
  between operations: 14 us -> 0.65 us
  starting transfers between devices: 0.01 us -> 8.89 us
  local copies, waits for them, and re-layouts: 26 us -> 30.7 us
    all_to_all x0 -> x2, waiting for transfers between devices: none -> 252 us  [the longest x1 243 us: body(): lax.all_to_all(jnp.stack([x_local for _ in range(lax.axis_size('chan'))])...]
    all_gather x1 -> x0, waiting for transfers between devices: 42.4 us -> none  [body(): lax.all_gather(out_weight, 'chan', axis=1, tiled=True)]
    all_to_all x1 -> x0, blocking collectives: 18.8 us -> none  [body(): lax.all_to_all(normed, 'chan', split_axis=0, concat_axis=1, tiled=True)]
    all_to_all x0 -> x2, starting transfers between devices: none -> 8.89 us  [the longest x1 5.13 us: body(): lax.all_to_all(jnp.stack([x_local for _ in range(lax.axis_size('chan'))])...]
    another operation x11 -> x12, local copies, waits for them, and re-layouts: 0.62 us -> 6.52 us  [the longest x1 5.91 us: body(): jnp.stack([x_local for _ in range(lax.axis_size('chan'))])]
  transfers between devices with their start and end apart: 1 -> 2, of which waited for: 1 -> 2; matrix products, arithmetic and copies ran while one was open for 32% -> 0% of each run, Pallas kernels for 0% -> 0%
where the time goes in v1:
time: 360 us; the launch traced here: 359 us
  waiting for transfers between devices  252 us (70%)
  blocking collectives  31.7 us (9%)
  local copies, waits for them, and re-layouts  30.7 us (9%)
  matrix products  19 us (5%)
  other arithmetic  15.7 us (4%)
  starting transfers between devices  8.89 us (2%)
    all_to_all x1, waiting for transfers between devices, body(): lax.all_to_all(jnp.stack([x_local for _ in range(lax.axis_size('chan'))])...  243 us
    all_to_all x1, blocking collectives, body(): lax.all_to_all(projected, 'chan', split_axis=1, concat_axis=0, tiled=True)  15.2 us
    all_to_all x1, blocking collectives, copy_for_each(): return lax.all_to_all(copies, axis, split_axis=0, concat_axis=0, tiled=True)  14.5 us
    dot_general x1, matrix products, body(): jnp.dot(frame_share, follow_bench(out_weight), preferred_element_type=jnp...  11 us
    another operation x8, other arithmetic  9.89 us
    all_to_all x1, waiting for transfers between devices, body(): lax.all_to_all(normed, 'chan', split_axis=0, concat_axis=1, tiled=True)  9.21 us
  transfers between devices with their start and end apart: 2, of which 2 were waited for; matrix products, arithmetic and copies ran while one was open for 0% of the time, Pallas kernels for 0%

profile of v1, /device:TPU:96, one launch (start us, length us, event | category | flops | bytes accessed | tf_op | source)
XLA Modules:
  0.0 359.0 jit_solution(18161798572122859605)
XLA Ops:
  0.1 1.3 copy.173
  1.4 6.3 %rev.17 = bf16[1024,256]{1,0:T(8,128)(2,1)S(1)} reverse(bf16[1024,256]{1,0:T(8,128)(2,1)} %param.15), dimensions={0} | reverse | bytes 1048576 | tf_op jit(solution)/shard_map/rev | solution.py:97
  7.7 0.8 negate_bitcast_fusion
  8.5 0.7 slice.57
  9.2 0.8 compare_select_fusion
  10.0 0.7 rev.15
  10.9 4.8 %reduce-window.14 = f32[4,4,2,128]{3,2,1,0:T(2,128)S(1)} reduce-window(f32[4,4,2,128]{3,2,1,0:T(2,128)S(1)} %reshape.304, f32[]{:T(128)} %constant.83.clone.1), window={size=1x1x1x128 pad=0_0x0_0x0_0x127_0}, to_apply=%region_0.1 | reduce-window | flops 520192 | bytes 32772 | tf_op jit(solution)/shard_map/reduce-window
  16.5 4.8 %reduce-window.16 = f32[4,4,2,128]{3,2,1,0:T(2,128)S(1)} reduce-window(f32[4,4,2,128]{3,2,1,0:T(2,128)S(1)} %reshape.308, f32[]{:T(128)} %constant.83.clone.1), window={size=1x1x1x128 pad=0_0x0_0x0_0x127_0}, to_apply=%region_6.7 | reduce-window | flops 520192 | bytes 32772 | tf_op jit(solution)/shard_map/reduce-window.2
  22.4 1.2 reshape.306
  24.5 0.7 fusion.56
  25.3 0.7 exponential_multiply_fusion.1
  25.9 1.8 convolution_bitcast_fusion.3
  28.5 1.2 slice_bitcast_fusion
  30.1 1.0 convolution_bitcast_fusion.2
  31.9 2.0 all_gather.3
  35.6 2.1 copy.188
  38.9 1.4 fusion.22
  40.7 0.7 copy.186
  41.6 1.5 rev.19
  43.5 2.5 fusion.23
  46.4 0.7 copy.184
  48.0 14.5 %all_to_all.50 = f32[16,1,1024]{2,1,0:T(1,128)S(1)} all-to-all(f32[16,1,1024]{2,1,0:T(1,128)S(1)} %broadcast_in_dim.57), channel_id=1, replica_groups=mesh['seq'=2,'chan'=16,'batch'=8] {'chan'}, dimensions={0} | all-to-all | bytes 131072 | tf_op jit(solution)/shard_map/all_to_all | solution.py:23
  62.7 1.0 copy.190
  63.7 3.8 %all-to-all-start.1 = ((bf16[16,64,256]{2,1,0:T(8,128)(2,1)}), bf16[16,64,256]{2,1,0:T(8,128)(2,1)S(1)}, u32[]{:S(2)}, u32[]{:S(2)}) async-start(bf16[16,64,256]{2,1,0:T(8,128)(2,1)} %bitcast.34), calls=%async_computation.1 | async-start | bytes 1048576 | tf_op jit(solution)/shard_map/all_to_all | solution.py:146
  67.4 1.5 copy.192
  68.9 9.2 %all-to-all-done.1 = bf16[16,64,256]{2,1,0:T(8,128)(2,1)S(1)} async-done(((bf16[16,64,256]{2,1,0:T(8,128)(2,1)}), bf16[16,64,256]{2,1,0:T(8,128)(2,1)S(1)}, u32[]{:S(2)}, u32[]{:S(2)}) %all-to-all-start.1) | async-done | bytes 524320 | tf_op jit(solution)/shard_map/all_to_all | solution.py:146
  78.1 5.9 %stack.20 = bf16[16,4096,128]{1,2,0:T(8,128)(2,1)} broadcast(bf16[4096,128]{0,1:T(8,128)(2,1)S(1)} %copy.192), dimensions={1,2} | broadcast | bytes 17825792 | tf_op jit(solution)/shard_map/stack | solution.py:148
  84.0 5.1 %all-to-all-start.2 = ((bf16[16,4096,128]{1,2,0:T(8,128)(2,1)}), bf16[16,4096,128]{1,2,0:T(8,128)(2,1)}, u32[]{:S(2)}, u32[]{:S(2)}) async-start(bf16[16,4096,128]{1,2,0:T(8,128)(2,1)} %stack.20), calls=%async_computation.2 | async-start | bytes 33554432 | tf_op jit(solution)/shard_map/all_to_all | solution.py:148
  89.2 242.9 %all-to-all-done.2 = bf16[16,4096,128]{1,2,0:T(8,128)(2,1)} async-done(((bf16[16,4096,128]{1,2,0:T(8,128)(2,1)}), bf16[16,4096,128]{1,2,0:T(8,128)(2,1)}, u32[]{:S(2)}, u32[]{:S(2)}) %all-to-all-start.2) | async-done | bytes 16777248 | tf_op jit(solution)/shard_map/all_to_all | solution.py:148
  332.1 11.0 %fusion.28 = bf16[8,16,8,128]{3,2,1,0:T(8,128)(2,1)S(1)} fusion(bf16[64,4096]{1,0:T(8,128)(2,1)S(1)} %bitcast.162, bf16[4096,2048]{0,1:T(8,128)(2,1)} %bitcast.37), kind=kOutput, calls=%fused_computation.49 | convolution fusion | flops 1073872896 | bytes 17563648 | tf_op jit(solution)/shard_map/dot_general | solution.py:150
  343.1 15.2 %all_to_all.49 = bf16[64,16,128]{2,0,1:T(8,128)(2,1)S(1)} all-to-all(bf16[64,16,128]{2,0,1:T(8,128)(2,1)S(1)} %bitcast.164), channel_id=1, replica_groups=mesh['seq'=2,'chan'=16,'batch'=8] {'chan'}, dimensions={1} | all-to-all | bytes 524288 | tf_op jit(solution)/shard_map/all_to_all | solution.py:153
  358.3 0.7 copy.248
  (133 shorter events, 11.0 us)
Async XLA Ops:
  0.0 24.5 %copy-start.8 = (bf16[2,1024,128]{2,1,0:T(8,128)(2,1)S(1)}, bf16[2,1024,128]{2,1,0:T(8,128)(2,1)}, u32[]{:S(2)}) copy-start(bf16[2,1024,128]{2,1,0:T(8,128)(2,1)} %param.17) | copy-start | bytes 1572868
  0.0 38.9 %copy-start.9 = (pred[256,256]{1,0:T(8,128)(4,1)}, pred[256,256]{1,0:T(8,128)(4,1)S(1)}, u32[]{:S(2)}) copy-start(pred[256,256]{1,0:T(8,128)(4,1)S(1)} %iota_compare_fusion) | copy-start | bytes 196612
  10.9 17.0 %copy-start.11 = (f32[4,4,256]{2,1,0:T(4,128)}, f32[4,4,256]{2,1,0:T(4,128)S(1)}, u32[]{:S(2)}) copy-start(f32[4,4,256]{2,1,0:T(4,128)S(1)} %get-tuple-element.314) | copy-start | bytes 49156
  25.2 4.8 %copy-start = (bf16[1,1024,128]{2,1,0:T(8,128)(2,1)}, bf16[1,1024,128]{2,1,0:T(8,128)(2,1)S(1)}, u32[]{:S(2)}) copy-start(bf16[1,1024,128]{2,1,0:T(8,128)(2,1)S(1)} %get-tuple-element.321) | copy-start | bytes 786436
  28.4 1.6 copy-start.3
  30.0 4.3 %copy-start.17 = (f32[4]{0:T(128)S(1)}, f32[4]{0:T(128)}, u32[]{:S(2)}) copy-start(f32[4]{0:T(128)} %param.21) | copy-start | bytes 52
  31.7 2.2 copy-start.5
  38.9 1.4 copy-start.6
  40.3 2.8 copy-start.1
  40.3 2.8 copy-start.2
  40.7 2.7 copy-start.10
  40.7 2.7 copy-start.12
  43.5 2.6 copy-start.4
  43.5 2.6 copy-start.13
  43.5 2.6 copy-start.14
  46.0 1.3 copy-start.7
  46.0 1.3 copy-start.15
  46.4 16.1 %copy-start.16 = (f32[256]{0:T(256)S(1)}, f32[256]{0:T(256)}, u32[]{:S(2)}) copy-start(f32[256]{0:T(256)} %param.22) | copy-start | bytes 3076
  63.7 14.5 %all-to-all-start.1 = ((bf16[16,64,256]{2,1,0:T(8,128)(2,1)}), bf16[16,64,256]{2,1,0:T(8,128)(2,1)S(1)}, u32[]{:S(2)}, u32[]{:S(2)}) async-start(bf16[16,64,256]{2,1,0:T(8,128)(2,1)} %bitcast.34), calls=%async_computation.1 | async-start | bytes 1048576 | tf_op jit(solution)/shard_map/all_to_all | solution.py:146
  84.0 248.1 %all-to-all-start.2 = ((bf16[16,4096,128]{1,2,0:T(8,128)(2,1)}), bf16[16,4096,128]{1,2,0:T(8,128)(2,1)}, u32[]{:S(2)}, u32[]{:S(2)}) async-start(bf16[16,4096,128]{1,2,0:T(8,128)(2,1)} %stack.20), calls=%async_computation.2 | async-start | bytes 33554432 | tf_op jit(solution)/shard_map/all_to_all | solution.py:148
